TPU v7x, 512 devices: a whole 4x8x8 slice. The times are simulated.
512 devices in a mesh: ket: 128 (over z, y, core), blk: 4 (over x).
Axes of the slice: x: 4, y: 8, z: 8, core: 2. Of those that a mesh axis runs over, the one named last changes fastest.
Arguments:
- density: float32 [8192, 64, 128], P('ket', 'blk'), may hold values from -24 to 24
- decay_matrix: float32 [128, 128], replicated, may hold values from -0.25 to 2, as said below
- atom_order: int32 [128], replicated, may hold values from 0 to 127, each once
Outputs:
- next_vector: float32 [8192, 64, 128], P('ket', 'blk')
- krylov_coeffs: float32 [5], replicated
- jump_flux: float32 [8192], P(('ket', 'blk'))
Inputs may be any that keep to these rules, and one draw needn't show every extreme that they name: `decay_matrix`: symmetric; diagonal entries from 0.5 to 2, off-diagonal entries at most 0.25 in magnitude. `atom_order`: each atom once.
All inputs are finite; a program needn't handle non-finite values.
Results may differ from a plain program's by a relative error of at most 0.0003.
Values sent between devices are 32-bit elements; how exact they have to be, the bound alone decides.
No kernel may reach another device: no remote copies, remote signals or barrier semaphores. Data moves between devices by JAX's collectives and lax.ppermute only.
A program may use at most 64 MiB of HBM per device.

v0:
```python
import jax
import jax.numpy as jnp
from jax import lax
from jax.sharding import PartitionSpec as P

highest = lax.Precision.HIGHEST


def shards(density, decay_matrix, atom_order):
    pair_rows, bra_local, atom_count = density.shape
    block_shape = density.shape
    half = bra_local * lax.axis_size("blk")
    entries = float(atom_count) * float(half) * float(half) * float(atom_count)
    onehot = (atom_order[:, None] == jnp.arange(atom_count)[None, :]).astype(jnp.float32)
    coupling = jnp.dot(
        jnp.dot(onehot, decay_matrix, precision=highest), onehot.T, precision=highest
    )
    window = coupling[:half, :half]

    def ket_part(turned):
        ket_cube = turned.reshape(atom_count, half, -1)
        summed = jnp.einsum("ia,ajc->ijc", coupling, ket_cube, precision=highest) + jnp.einsum(
            "jb,ibc->ijc", window, ket_cube, precision=highest
        )
        return summed.reshape(turned.shape)

    def bra_part(tensor):
        turned = lax.all_to_all(tensor, "blk", split_axis=2, concat_axis=1, tiled=True)
        mixed_rows = jnp.einsum("kb,pbc->pkc", window, turned, precision=highest)
        returned = lax.all_to_all(mixed_rows, "blk", split_axis=1, concat_axis=2, tiled=True)
        return returned + jnp.einsum("ld,pkd->pkl", coupling, tensor, precision=highest)

    def krylov_step(vectors, image_vec):
        local_dots = jnp.stack([jnp.sum(vector * image_vec) for vector in vectors])
        correlation = lax.psum(local_dots, ("ket", "blk")) / entries
        residual = image_vec
        for position in range(len(vectors)):
            residual = residual - correlation[position] * vectors[position]
        length_value = jnp.sqrt(lax.psum(jnp.sum(residual * residual), ("ket", "blk")) / entries)
        return (correlation, length_value, residual / length_value)

    norm_start = lax.psum(jnp.sum(density * density), ("ket", "blk"))
    vector_one = density / jnp.sqrt(norm_start / entries)

    def liouvillian(tensor):
        turned = lax.all_to_all(
            tensor.reshape(pair_rows, -1), "ket", split_axis=1, concat_axis=0, tiled=True
        )
        returned = lax.all_to_all(
            ket_part(turned), "ket", split_axis=0, concat_axis=1, tiled=True
        ).reshape(block_shape)
        return -0.5 * (returned + bra_part(tensor))

    coeff_one, length_one, vector_two = krylov_step([vector_one], liouvillian(vector_one))
    coeff_two, length_two, next_vector = krylov_step(
        [vector_one, vector_two], liouvillian(vector_two)
    )
    krylov_coeffs = jnp.concatenate([coeff_one, length_one[None], coeff_two, length_two[None]])
    pair_start = lax.axis_index("ket") * pair_rows
    pair_ids = pair_start + jnp.arange(pair_rows, dtype=jnp.int32)
    row_atoms = pair_ids // half
    picker = (row_atoms[:, None] == jnp.arange(atom_count)[None, :]).astype(jnp.float32)
    rows_full = jnp.dot(picker, coupling[:, :half], precision=highest)
    weights = lax.dynamic_slice_in_dim(rows_full, lax.axis_index("blk") * bra_local, bra_local, 1)
    summed_rows = jnp.einsum("pb,pbl->pl", weights, density, precision=highest)
    partial_value = summed_rows.reshape(pair_rows // half, half, atom_count).sum(0)
    jump_flux = lax.psum_scatter(
        partial_value.reshape(-1) / atom_count, ("ket", "blk"), scatter_dimension=0, tiled=True
    )
    return (next_vector, krylov_coeffs, jump_flux)


def solution(mesh):
    return jax.shard_map(
        shards,
        mesh=mesh,
        in_specs=(P("ket", "blk", None), P(), P()),
        out_specs=(P("ket", "blk", None), P(), P(("ket", "blk"))),
        check_vma=False,
    )
```

profile of v0, /device:TPU:1, one launch (start us, length us, event | category | flops | bytes accessed | tf_op | source)
XLA Modules:
  0.0 683.7 jit_solution(7631907614733165362)
XLA Ops:
  0.7 1.8 multiply_reduce_fusion.5
  2.5 106.1 %psum.35 = f32[]{:T(128)} all-reduce(f32[]{:T(128)} %multiply_reduce_fusion.5), channel_id=1, replica_groups=mesh['ket'=128,'blk'=4] {'ket','blk'}, use_global_device_ids=true, to_apply=%region_1.0 | all-reduce | flops 1 | bytes 8 | tf_op jit(solution)/shard_map/psum | solution.py:42
  109.9 1.4 reshape.81
  111.4 3.5 all-to-all-start.2
  115.2 1.5 reshape.77
  116.7 7.1 %all-to-all-done.2 = f32[4,1,32768]{2,1,0:T(1,128)S(1)} async-done(((f32[4,1,32768]{2,1,0:T(1,128)}), f32[4,1,32768]{2,1,0:T(1,128)S(1)}, u32[]{:S(2)}, u32[]{:S(2)}) %all-to-all-start.2) | async-done | bytes 524320 | tf_op jit(solution)/shard_map/all_to_all | solution.py:28
  123.7 10.5 %all-to-all-start = ((f32[128,1,1024]{2,1,0:T(1,128)}), f32[128,1,1024]{2,1,0:T(1,128)}, u32[]{:S(2)}, u32[]{:S(2)}) async-start(f32[128,1,1024]{2,1,0:T(1,128)} %reshape.77), calls=%async_computation | async-start | bytes 1048576 | tf_op jit(solution)/shard_map/all_to_all | solution.py:46
  135.3 2.1 reduce.2
  138.3 2.2 convolution_bitcast_fusion.1
  141.4 1.5 reshape.83
  142.9 11.6 %all-to-all-done = f32[128,1,1024]{2,1,0:T(1,128)} async-done(((f32[128,1,1024]{2,1,0:T(1,128)}), f32[128,1,1024]{2,1,0:T(1,128)}, u32[]{:S(2)}, u32[]{:S(2)}) %all-to-all-start) | async-done | bytes 524320 | tf_op jit(solution)/shard_map/all_to_all | solution.py:46
  154.5 4.3 all-to-all-start.3
  158.8 2.9 reduce
  164.1 1.4 reshape.79
  165.6 3.2 all-to-all-done.3
  168.8 6.7 all-to-all-start.1
  175.5 3.1 reduce.3
  180.3 15.5 %all-to-all-done.1 = f32[128,1,1024]{2,1,0:T(1,128)} async-done(((f32[128,1,1024]{2,1,0:T(1,128)}), f32[128,1,1024]{2,1,0:T(1,128)}, u32[]{:S(2)}, u32[]{:S(2)}) %all-to-all-start.1) | async-done | bytes 524320 | tf_op jit(solution)/shard_map/all_to_all | solution.py:49
  195.8 2.9 reduce.1
  201.3 93.5 %psum.36 = f32[1]{0:T(128)} all-reduce(f32[1]{0:T(128)} %bitcast.18), channel_id=1, replica_groups=mesh['ket'=128,'blk'=4] {'ket','blk'}, use_global_device_ids=true, to_apply=%region_3.0 | all-reduce | flops 1 | bytes 8 | tf_op jit(solution)/shard_map/psum | solution.py:35
  296.2 95.6 %psum.37 = f32[]{:T(128)} all-reduce(f32[]{:T(128)} %multiply_reduce_fusion.3), channel_id=1, replica_groups=mesh['ket'=128,'blk'=4] {'ket','blk'}, use_global_device_ids=true, to_apply=%region_5.0 | all-reduce | flops 1 | bytes 8 | tf_op jit(solution)/shard_map/psum | solution.py:39
  393.2 1.4 reshape.89
  394.6 3.5 all-to-all-start.6
  398.5 1.5 reshape.85
  399.9 7.1 %all-to-all-done.6 = f32[4,1,32768]{2,1,0:T(1,128)S(1)} async-done(((f32[4,1,32768]{2,1,0:T(1,128)}), f32[4,1,32768]{2,1,0:T(1,128)S(1)}, u32[]{:S(2)}, u32[]{:S(2)}) %all-to-all-start.6) | async-done | bytes 524320 | tf_op jit(solution)/shard_map/all_to_all | solution.py:28
  407.8 10.1 %all-to-all-start.4 = ((f32[128,1,1024]{2,1,0:T(1,128)}), f32[128,1,1024]{2,1,0:T(1,128)}, u32[]{:S(2)}, u32[]{:S(2)}) async-start(f32[128,1,1024]{2,1,0:T(1,128)} %reshape.85), calls=%async_computation.4 | async-start | bytes 1048576 | tf_op jit(solution)/shard_map/all_to_all | solution.py:46
  417.8 3.1 reduce.6
  421.8 2.2 convolution_bitcast_fusion
  424.0 1.8 copy.103
  425.7 2.7 reshape.91
  428.4 9.6 %all-to-all-done.4 = f32[128,1,1024]{2,1,0:T(1,128)} async-done(((f32[128,1,1024]{2,1,0:T(1,128)}), f32[128,1,1024]{2,1,0:T(1,128)}, u32[]{:S(2)}, u32[]{:S(2)}) %all-to-all-start.4) | async-done | bytes 524320 | tf_op jit(solution)/shard_map/all_to_all | solution.py:46
  438.1 4.3 all-to-all-start.7
  442.4 2.9 reduce.4
  446.6 1.4 fusion.1
  448.0 1.5 copy.97
  449.5 1.4 reshape.87
  451.0 1.4 all-to-all-done.7
  452.4 6.7 all-to-all-start.5
  460.0 3.1 reduce.7
  464.7 1.6 copy.106
  466.3 13.1 %all-to-all-done.5 = f32[128,1,1024]{2,1,0:T(1,128)} async-done(((f32[128,1,1024]{2,1,0:T(1,128)}), f32[128,1,1024]{2,1,0:T(1,128)}, u32[]{:S(2)}, u32[]{:S(2)}) %all-to-all-start.5) | async-done | bytes 524320 | tf_op jit(solution)/shard_map/all_to_all | solution.py:49
  479.4 3.7 reduce.5
  483.1 1.3 reshape.88
  485.6 2.3 multiply_reduce_fusion.2
  487.9 1.4 pad_maximum_fusion
  489.2 93.6 %psum.38 = f32[2]{0:T(128)S(1)} all-reduce(f32[2]{0:T(128)S(1)} %pad_maximum_fusion), channel_id=1, replica_groups=mesh['ket'=128,'blk'=4] {'ket','blk'}, use_global_device_ids=true, to_apply=%region_8.0 | all-reduce | flops 2 | bytes 16 | tf_op jit(solution)/shard_map/psum | solution.py:35
  583.4 2.0 multiply_reduce_fusion
  585.4 95.4 %all-reduce.1 = (f32[]{:T(128)}, f32[8192]{0:T(1024)S(1)}) all-reduce(f32[]{:T(128)} %get-tuple-element.7, f32[8192]{0:T(1024)S(1)} %multiply_bitcast_fusion), channel_id=1, replica_groups=mesh['ket'=128,'blk'=4] {'ket','blk'}, use_global_device_ids=true, to_apply=%region_10.0 | all-reduce | flops 8193 | bytes 65544 | tf_op jit(solution)/shard_map/psum | solution.py:39
  (53 shorter events, 21.3 us)
Async XLA Ops:
  0.6 133.6 %copy-start = (f32[128,128]{1,0:T(8,128)S(1)}, f32[128,128]{1,0:T(8,128)}, u32[]{:S(2)}) copy-start(f32[128,128]{1,0:T(8,128)} %param.4) | copy-start | bytes 196612
  0.6 108.6 %copy-start.1 = (f32[64,16,128]{2,1,0:T(8,128)S(1)}, f32[64,16,128]{2,1,0:T(8,128)}, u32[]{:S(2)}) copy-start(f32[64,16,128]{2,1,0:T(8,128)} %param.3) | copy-start | bytes 1572868
  111.4 12.3 %all-to-all-start.2 = ((f32[4,1,32768]{2,1,0:T(1,128)}), f32[4,1,32768]{2,1,0:T(1,128)S(1)}, u32[]{:S(2)}, u32[]{:S(2)}) async-start(f32[4,1,32768]{2,1,0:T(1,128)} %reshape.81), calls=%async_computation.2 | async-start | bytes 1048576 | tf_op jit(solution)/shard_map/all_to_all | solution.py:28
  116.7 17.6 %copy-start.4 = (s32[128]{0:T(128)S(1)}, s32[128]{0:T(128)}, u32[]{:S(2)}) copy-start(s32[128]{0:T(128)} %param.5) | copy-start | bytes 1540
  123.7 30.7 %all-to-all-start = ((f32[128,1,1024]{2,1,0:T(1,128)}), f32[128,1,1024]{2,1,0:T(1,128)}, u32[]{:S(2)}, u32[]{:S(2)}) async-start(f32[128,1,1024]{2,1,0:T(1,128)} %reshape.77), calls=%async_computation | async-start | bytes 1048576 | tf_op jit(solution)/shard_map/all_to_all | solution.py:46
  154.5 14.3 %all-to-all-start.3 = ((f32[4,1,32768]{2,1,0:T(1,128)}), f32[4,1,32768]{2,1,0:T(1,128)}, u32[]{:S(2)}, u32[]{:S(2)}) async-start(f32[4,1,32768]{2,1,0:T(1,128)} %reshape.83), calls=%async_computation.3 | async-start | bytes 1048576 | tf_op jit(solution)/shard_map/all_to_all | solution.py:30
  168.8 27.0 %all-to-all-start.1 = ((f32[128,1,1024]{2,1,0:T(1,128)}), f32[128,1,1024]{2,1,0:T(1,128)}, u32[]{:S(2)}, u32[]{:S(2)}) async-start(f32[128,1,1024]{2,1,0:T(1,128)} %reshape.79), calls=%async_computation.1 | async-start | bytes 1048576 | tf_op jit(solution)/shard_map/all_to_all | solution.py:49
  199.0 1.0 copy-start.2
  394.6 12.3 %all-to-all-start.6 = ((f32[4,1,32768]{2,1,0:T(1,128)}), f32[4,1,32768]{2,1,0:T(1,128)S(1)}, u32[]{:S(2)}, u32[]{:S(2)}) async-start(f32[4,1,32768]{2,1,0:T(1,128)} %reshape.89), calls=%async_computation.6 | async-start | bytes 1048576 | tf_op jit(solution)/shard_map/all_to_all | solution.py:28
  407.0 0.8 copy-start.3
  407.8 30.3 %all-to-all-start.4 = ((f32[128,1,1024]{2,1,0:T(1,128)}), f32[128,1,1024]{2,1,0:T(1,128)}, u32[]{:S(2)}, u32[]{:S(2)}) async-start(f32[128,1,1024]{2,1,0:T(1,128)} %reshape.85), calls=%async_computation.4 | async-start | bytes 1048576 | tf_op jit(solution)/shard_map/all_to_all | solution.py:46
  438.1 14.3 %all-to-all-start.7 = ((f32[4,1,32768]{2,1,0:T(1,128)}), f32[4,1,32768]{2,1,0:T(1,128)}, u32[]{:S(2)}, u32[]{:S(2)}) async-start(f32[4,1,32768]{2,1,0:T(1,128)} %reshape.91), calls=%async_computation.7 | async-start | bytes 1048576 | tf_op jit(solution)/shard_map/all_to_all | solution.py:30
  452.4 27.0 %all-to-all-start.5 = ((f32[128,1,1024]{2,1,0:T(1,128)}), f32[128,1,1024]{2,1,0:T(1,128)}, u32[]{:S(2)}, u32[]{:S(2)}) async-start(f32[128,1,1024]{2,1,0:T(1,128)} %reshape.87), calls=%async_computation.5 | async-start | bytes 1048576 | tf_op jit(solution)/shard_map/all_to_all | solution.py:49
where the time goes:
time: 693 us; the launch traced here: 684 us
  blocking collectives  484 us (70%)
  waiting for transfers between devices  68.6 us (10%)
  starting transfers between devices  49.5 us (7%)
  local copies, waits for them, and re-layouts  33.8 us (5%)
  other arithmetic  31.4 us (5%)
  matrix products  12.3 us (2%)
    psum x2, blocking collectives, krylov_step(): lax.psum(jnp.sum(residual * residual), ('ket', 'blk')) / entries  191 us
    psum x2, blocking collectives, krylov_step(): correlation = lax.psum(local_dots, ('ket', 'blk')) / entries  187 us
    psum x1, blocking collectives, shards(): norm_start = lax.psum(jnp.sum(density * density), ('ket', 'blk'))  106 us
    all_to_all x2, waiting for transfers between devices, liouvillian(): lax.all_to_all(ket_part(turned), 'ket', split_axis=0, concat_axis=1, tile...  28.6 us
    all_to_all x2, waiting for transfers between devices, liouvillian(): lax.all_to_all(tensor.reshape(pair_rows, -1), 'ket', split_axis=1, concat...  21.2 us
    all_to_all x2, starting transfers between devices, liouvillian(): lax.all_to_all(tensor.reshape(pair_rows, -1), 'ket', split_axis=1, concat...  20.6 us
    unnamed x27, local copies, waits for them, and re-layouts  19.1 us
    all_to_all x2, waiting for transfers between devices, bra_part(): lax.all_to_all(tensor, 'blk', split_axis=2, concat_axis=1, tiled=True)  14.1 us
  transfers between devices with their start and end apart: 8, of which 8 were waited for; matrix products, arithmetic and copies ran while one was open for 7% of the time, Pallas kernels for 0%

commit v1 on v0

v1 whole, which is shorter than its diff:
```python
import jax
import jax.numpy as jnp
from jax import lax
from jax.sharding import PartitionSpec as P

highest = lax.Precision.HIGHEST
both = ("ket", "blk")


def swap(rows):
    return lax.all_to_all(rows, both, split_axis=0, concat_axis=0, tiled=True)


def shards(density, decay_matrix, atom_order):
    pair_rows, bra_local, atom_count = density.shape
    blk = lax.axis_size("blk")
    devices = lax.axis_size("ket") * blk
    half = bra_local * blk
    own = half * atom_count // devices
    groups = atom_count // own
    entries = float(atom_count) * float(half) * float(half) * float(atom_count)
    onehot = (atom_order[:, None] == jnp.arange(atom_count)[None, :]).astype(jnp.float32)
    coupling = jnp.dot(
        jnp.dot(onehot, decay_matrix, precision=highest), onehot.T, precision=highest
    )
    window = coupling[:half, :half]
    mean_full = jnp.trace(coupling) / atom_count
    mean_half = jnp.trace(window) / half
    full_zero = coupling - mean_full * jnp.eye(atom_count, dtype=jnp.float32)
    half_zero = window - mean_half * jnp.eye(half, dtype=jnp.float32)
    shift = 2.0 * (mean_full + mean_half)

    def outer_terms(turned):
        return jnp.einsum("ia,akl->ikl", full_zero, turned, precision=highest) + jnp.einsum(
            "kb,ibl->ikl", half_zero, turned, precision=highest
        )

    def inner_terms(tensor):
        return jnp.einsum("jb,bkl->jkl", half_zero, tensor, precision=highest) + jnp.einsum(
            "ld,jkd->jkl", full_zero, tensor, precision=highest
        )

    sent = density.reshape(half, bra_local, groups, own).transpose(0, 2, 1, 3)
    turned = swap(sent.reshape(devices, bra_local * own)).reshape(atom_count, half, own)
    jump_flux = jnp.einsum("ik,ikl->l", coupling[:, :half], turned, precision=highest) / atom_count
    once = outer_terms(turned)
    twice = outer_terms(once)
    packed = jnp.stack(
        [once.reshape(devices, bra_local * own), twice.reshape(devices, bra_local * own)], axis=1
    )
    returned = swap(packed).reshape(half, groups, 2, bra_local, own).transpose(2, 0, 3, 1, 4)
    returned = returned.reshape((2,) + density.shape)
    once, twice = returned[0], returned[1]
    image_one = once + inner_terms(density)
    image_two = twice + inner_terms(once + image_one)
    local = jnp.stack(
        [
            jnp.sum(density * density),
            jnp.sum(density * image_one),
            jnp.sum(image_one * image_one),
            jnp.sum(image_one * image_two),
            jnp.sum(image_two * image_two),
        ]
    )
    shared = swap(jnp.broadcast_to(local[None, :], (devices, local.shape[0])))
    mom = jnp.sum(shared, axis=0) / entries
    ratio = mom[1] / mom[0]
    gap = mom[2] - ratio * mom[1]
    theta = (mom[3] - 2.0 * ratio * mom[2] + ratio * ratio * mom[1]) / gap
    slope = ratio + theta
    offset = theta * ratio - gap / mom[0]
    size = jnp.sqrt(mom[4] - slope * mom[3] + offset * mom[2])
    next_vector = (image_two - slope * image_one + offset * density) / size
    b_one = 0.5 * jnp.sqrt(gap / mom[0])
    krylov_coeffs = jnp.stack(
        [
            -0.5 * (ratio + shift),
            b_one,
            b_one,
            -0.5 * (theta + shift),
            0.5 * size / jnp.sqrt(gap),
        ]
    )
    return (next_vector, krylov_coeffs, jump_flux)


def solution(mesh):
    return jax.shard_map(
        shards,
        mesh=mesh,
        in_specs=(P("ket", "blk", None), P(), P()),
        out_specs=(P("ket", "blk", None), P(), P(("ket", "blk"))),
        check_vma=False,
    )
```

time: 693 us -> 191 us (0.28); the launches traced: 684 us -> 190 us
  blocking collectives: 484 us -> 0 us
  other arithmetic: 31.4 us -> 3.47 us
  local copies, waits for them, and re-layouts: 33.8 us -> 61.2 us
  starting transfers between devices: 49.5 us -> 41.6 us
  waiting for transfers between devices: 68.6 us -> 61.2 us
    psum x5 -> x0, blocking collectives: 484 us -> none  [the longest x2 191 us: krylov_step(): lax.psum(jnp.sum(residual * residual), ('ket', 'blk')) / entries]
    all_to_all x8 -> x1, other arithmetic: 23.8 us -> 1.24 us  [swap(): return lax.all_to_all(rows, both, split_axis=0, concat_axis=0, tiled=True)]
    unnamed x27 -> x8, local copies, waits for them, and re-layouts: 19.1 us -> 2.54 us
    slice x1 -> x6, local copies, waits for them, and re-layouts: 0.58 us -> 15.8 us  [the longest x3 15 us: shards(): once, twice = (returned[0], returned[1])]
    another operation x0 -> x5, local copies, waits for them, and re-layouts: none -> 12.6 us  [the longest x3 8.78 us: shards(): jnp.stack([once.reshape(devices, bra_local * own), twice.reshape(devices,...]
    reshape x2 -> x3, local copies, waits for them, and re-layouts: 1.53 us -> 11.2 us  [the longest x2 6.59 us: shards(): swap(sent.reshape(devices, bra_local * own)).reshape(atom_count, half, own)]
    all_to_all x8 -> x3, starting transfers between devices: 49.5 us -> 41.6 us  [swap(): return lax.all_to_all(rows, both, split_axis=0, concat_axis=0, tiled=True)]
    all_to_all x8 -> x3, waiting for transfers between devices: 68.6 us -> 61.2 us  [swap(): return lax.all_to_all(rows, both, split_axis=0, concat_axis=0, tiled=True)]
  transfers between devices with their start and end apart: 8 -> 3, of which waited for: 8 -> 3; matrix products, arithmetic and copies ran while one was open for 7% -> 4% of each run, Pallas kernels for 0% -> 0%
where the time goes in v1:
time: 191 us; the launch traced here: 190 us
  local copies, waits for them, and re-layouts  61.2 us (32%)
  waiting for transfers between devices  61.2 us (32%)
  starting transfers between devices  41.6 us (22%)
  matrix products  13.2 us (7%)
  between operations  9.42 us (5%)
  other arithmetic  3.47 us (2%)
    all_to_all x3, waiting for transfers between devices, swap(): return lax.all_to_all(rows, both, split_axis=0, concat_axis=0, tiled=True)  61.2 us
    all_to_all x3, starting transfers between devices, swap(): return lax.all_to_all(rows, both, split_axis=0, concat_axis=0, tiled=True)  41.6 us
    slice x3, local copies, waits for them, and re-layouts, shards(): once, twice = (returned[0], returned[1])  15 us
    add x2, local copies, waits for them, and re-layouts, outer_terms(): jnp.einsum('ia,akl->ikl', full_zero, turned, precision=highest)  8.81 us
    another operation x3, local copies, waits for them, and re-layouts, shards(): jnp.stack([once.reshape(devices, bra_local * own), twice.reshape(devices,...  8.78 us
    reshape x2, local copies, waits for them, and re-layouts, shards(): swap(sent.reshape(devices, bra_local * own)).reshape(atom_count, half, own)  6.59 us
    reshape x1, local copies, waits for them, and re-layouts, shards(): swap(packed).reshape(half, groups, 2, bra_local, own)  4.66 us
    transpose x1, local copies, waits for them, and re-layouts, shards(): sent = density.reshape(half, bra_local, groups, own).transpose(0, 2, 1, 3)  4.43 us
  transfers between devices with their start and end apart: 3, of which 3 were waited for; matrix products, arithmetic and copies ran while one was open for 4% of the time, Pallas kernels for 0%

profile of v1, /device:TPU:1, one launch (start us, length us, event | category | flops | bytes accessed | tf_op | source)
XLA Modules:
  0.0 190.0 jit_solution(3026357759136375597)
XLA Ops:
  0.6 0.0 copy-start
  0.6 1.4 copy.135
  2.1 0.0 copy-start.2
  2.1 4.4 %copy.136 = f32[64,8,16,16]{3,2,1,0:T(8,128)} copy(f32[64,8,16,16]{0,3,1,2:T(8,128)S(1)} %bitcast.81) | data formatting | bytes 1048576 | tf_op jit(solution)/shard_map/transpose | solution.py:43
  6.5 4.2 %all_to_all.17 = f32[512,1,256]{2,1,0:T(1,128)} reshape(f32[64,8,16,16]{3,2,1,0:T(8,128)} %copy.136) | data formatting | bytes 1048576 | tf_op jit(solution)/shard_map/all_to_all | solution.py:11
  10.7 22.2 %all-to-all-start = ((f32[512,1,256]{2,1,0:T(1,128)}), f32[512,1,256]{2,1,0:T(1,128)S(1)}, u32[]{:S(2)}, u32[]{:S(2)}) async-start(f32[512,1,256]{2,1,0:T(1,128)} %all_to_all.17), calls=%async_computation | async-start | bytes 1048576 | tf_op jit(solution)/shard_map/all_to_all | solution.py:11
  32.9 0.2 fusion.19
  33.1 0.8 select_reduce_fusion
  34.6 0.6 select_reduce_fusion.1
  35.9 18.2 %all-to-all-done = f32[512,1,256]{2,1,0:T(1,128)S(1)} async-done(((f32[512,1,256]{2,1,0:T(1,128)}), f32[512,1,256]{2,1,0:T(1,128)S(1)}, u32[]{:S(2)}, u32[]{:S(2)}) %all-to-all-start) | async-done | bytes 524320 | tf_op jit(solution)/shard_map/all_to_all | solution.py:11
  54.1 1.2 reduce.1
  55.4 2.6 %reshape.33 = f32[128,64,16]{2,1,0:T(8,128)} reshape(f32[512,256]{1,0:T(8,128)S(1)} %reduce.1) | data formatting | bytes 1048576 | tf_op jit(solution)/shard_map/reshape | solution.py:44
  58.0 3.9 %copy.139 = f32[128,64,16]{0,1,2:T(8,128)S(1)} copy(f32[128,64,16]{2,1,0:T(8,128)} %reshape.33) | data formatting | bytes 1048576 | tf_op jit(solution)/shard_map/reshape | solution.py:44
  62.0 0.6 fusion.16
  62.6 0.6 fusion
  63.2 0.6 fusion.14
  63.8 4.4 %copy.142 = f32[128,64,16]{2,1,0:T(8,128)} copy(f32[128,64,16]{0,1,2:T(8,128)S(1)} %fusion) | data formatting | bytes 1048576 | tf_op jit(solution)/shard_map/add | solution.py:34
  68.2 0.6 fusion.1
  68.8 3.5 %stack_reshape.6 = f32[512,1,256]{2,0,1:T(8,128)S(1)} reshape(f32[128,64,16]{2,1,0:T(8,128)} %copy.142) | data formatting | bytes 1048576 | tf_op jit(solution)/shard_map/stack;reshape | solution.py:48
  72.3 4.4 %copy.145 = f32[128,64,16]{2,1,0:T(8,128)} copy(f32[128,64,16]{0,1,2:T(8,128)S(1)} %fusion.1) | data formatting | bytes 1048576 | tf_op jit(solution)/shard_map/add | solution.py:34
  76.7 3.5 %stack_reshape.7 = f32[512,1,256]{2,0,1:T(8,128)S(1)} reshape(f32[128,64,16]{2,1,0:T(8,128)} %copy.145) | data formatting | bytes 1048576 | tf_op jit(solution)/shard_map/stack;reshape | solution.py:48
  80.2 0.1 pad_maximum_fusion
  80.3 1.8 copy.146
  82.1 10.0 %all-to-all-start.1 = ((f32[512,2,256]{2,1,0:T(2,128)}), f32[512,2,256]{2,1,0:T(2,128)S(1)}, u32[]{:S(2)}, u32[]{:S(2)}) async-start(f32[512,2,256]{2,1,0:T(2,128)} %copy.146), calls=%async_computation.1 | async-start | bytes 2097152 | tf_op jit(solution)/shard_map/all_to_all | solution.py:11
  92.2 0.1 copy.175
  92.3 0.8 multiply_reduce_fusion.4
  93.0 0.7 fusion.7
  93.8 30.9 %all-to-all-done.1 = f32[512,2,256]{2,1,0:T(2,128)S(1)} async-done(((f32[512,2,256]{2,1,0:T(2,128)}), f32[512,2,256]{2,1,0:T(2,128)S(1)}, u32[]{:S(2)}, u32[]{:S(2)}) %all-to-all-start.1) | async-done | bytes 1048608 | tf_op jit(solution)/shard_map/all_to_all | solution.py:11
  124.7 0.1 copy.147
  124.8 4.7 %reshape.34 = f32[64,8,2,16,16]{4,3,1,0,2:T(8,128)} reshape(f32[512,2,256]{2,0,1:T(8,128)S(1)} %copy.147) | data formatting | bytes 2097152 | tf_op jit(solution)/shard_map/reshape | solution.py:51
  129.5 7.8 %fusion.34 = (f32[1,64,16,8,16]{4,2,3,1,0:T(8,128)}, f32[1,64,16,8,16]{4,2,3,1,0:T(8,128)}) fusion(f32[2,64,16,8,16]{4,2,3,1,0:T(8,128)} %bitcast.78), kind=kLoop, calls=%fused_computation.55 | loop fusion | bytes 2097152 | tf_op jit(solution)/shard_map/slice | solution.py:53
  137.2 3.6 %copy.149 = f32[1,64,16,8,16]{1,4,3,2,0:T(8,128)S(1)} copy(f32[1,64,16,8,16]{4,2,3,1,0:T(8,128)} %get-tuple-element.25) | data formatting | bytes 1048576 | tf_op jit(solution)/shard_map/slice | solution.py:53
  140.9 0.3 copy.155
  141.2 0.7 fusion.3
  141.9 1.4 fusion.10
  143.3 3.6 %copy.148 = f32[1,64,16,8,16]{1,4,3,2,0:T(8,128)S(1)} copy(f32[1,64,16,8,16]{4,2,3,1,0:T(8,128)} %get-tuple-element.26) | data formatting | bytes 1048576 | tf_op jit(solution)/shard_map/slice | solution.py:53
  146.9 0.3 copy.160
  147.2 2.5 %multiply_reduce_fusion = (f32[]{:T(128)}, f32[]{:T(128)}, f32[]{:T(128)}, f32[]{:T(128)}, f32[64,16,128]{2,0,1:T(8,128)S(1)}) fusion(f32[64,16,128]{2,0,1:T(8,128)S(1)} %fusion.3, f32[64,16,128]{2,1,0:T(8,128)S(1)} %copy-done.1, f32[64,16,128]{2,0,1:T(8,128)S(1)} %copy.160, f32[64,16,128]{2,0,1:T(8,128)} %fusion.10, f32[128,128]{0,1:T(8,128)S(1)} %get-tuple-element.33, ...), kind=kOutput, calls=%fused_computation.13 | convolution fusion | flops 202817536 | bytes 3211284 | tf_op jit(solution)/shard_map/ld,jkd->jkl/dot_general | solution.py:39
  149.7 3.2 %stack.43 = f32[5]{0:T(128)S(1)} concatenate(f32[1]{0:T(128)} %bitcast.16, f32[1]{0:T(128)} %bitcast.17, f32[1]{0:T(128)} %bitcast.18, f32[1]{0:T(128)} %bitcast.19, f32[1]{0:T(128)} %bitcast.20), dimensions={0} | concatenate | bytes 40 | tf_op jit(solution)/shard_map/stack | solution.py:56
  152.9 0.8 broadcast_in_dim.18
  153.8 9.4 %all-to-all-start.2 = ((f32[512,1,5]{2,1,0:T(1,128)}), f32[512,1,5]{2,1,0:T(1,128)S(1)}, u32[]{:S(2)}, u32[]{:S(2)}) async-start(f32[512,1,5]{2,1,0:T(1,128)} %broadcast_in_dim.18), calls=%async_computation.2 | async-start | bytes 524288 | tf_op jit(solution)/shard_map/all_to_all | solution.py:11
  163.2 4.4 %fusion.5 = f32[16]{0:T(128)} fusion(f32[128,64,1]{1,2,0:T(1,128)S(1)} %copy.175, f32[128,64,16]{2,1,0:T(8,128)} %reshape.33), kind=kOutput, calls=%fused_computation.10 | convolution fusion | flops 1572880 | bytes 557120 | tf_op jit(solution)/shard_map/ik,ikl->l/dot_general | solution.py:45
  167.6 12.0 %all-to-all-done.2 = f32[512,1,5]{2,1,0:T(1,128)S(1)} async-done(((f32[512,1,5]{2,1,0:T(1,128)}), f32[512,1,5]{2,1,0:T(1,128)S(1)}, u32[]{:S(2)}, u32[]{:S(2)}) %all-to-all-start.2) | async-done | bytes 10272 | tf_op jit(solution)/shard_map/all_to_all | solution.py:11
  179.6 0.6 reduce_sum.81
  180.1 0.7 fusion.35
  188.1 0.2 add_divide_fusion
  188.3 1.1 copy.164
  189.4 0.6 stack.48
  (6 shorter events, 0.0 us)
Async XLA Ops:
  0.6 32.2 %copy-start = (f32[128,128]{1,0:T(8,128)S(1)}, f32[128,128]{1,0:T(8,128)}, u32[]{:S(2)}) copy-start(f32[128,128]{1,0:T(8,128)} %param.4) | copy-start | bytes 196612
  2.1 30.8 %copy-start.2 = (s32[128]{0:T(128)S(1)}, s32[128]{0:T(128)}, u32[]{:S(2)}) copy-start(s32[128]{0:T(128)} %param.5) | copy-start | bytes 1540
  10.7 43.4 %all-to-all-start = ((f32[512,1,256]{2,1,0:T(1,128)}), f32[512,1,256]{2,1,0:T(1,128)S(1)}, u32[]{:S(2)}, u32[]{:S(2)}) async-start(f32[512,1,256]{2,1,0:T(1,128)} %all_to_all.17), calls=%async_computation | async-start | bytes 1048576 | tf_op jit(solution)/shard_map/all_to_all | solution.py:11
  80.2 12.1 %copy-start.1 = (f32[64,16,128]{2,1,0:T(8,128)S(1)}, f32[64,16,128]{2,1,0:T(8,128)}, u32[]{:S(2)}) copy-start(f32[64,16,128]{2,1,0:T(8,128)} %param.3) | copy-start | bytes 1572868
  82.1 42.6 %all-to-all-start.1 = ((f32[512,2,256]{2,1,0:T(2,128)}), f32[512,2,256]{2,1,0:T(2,128)S(1)}, u32[]{:S(2)}, u32[]{:S(2)}) async-start(f32[512,2,256]{2,1,0:T(2,128)} %copy.146), calls=%async_computation.1 | async-start | bytes 2097152 | tf_op jit(solution)/shard_map/all_to_all | solution.py:11
  153.8 25.8 %all-to-all-start.2 = ((f32[512,1,5]{2,1,0:T(1,128)}), f32[512,1,5]{2,1,0:T(1,128)S(1)}, u32[]{:S(2)}, u32[]{:S(2)}) async-start(f32[512,1,5]{2,1,0:T(1,128)} %broadcast_in_dim.18), calls=%async_computation.2 | async-start | bytes 524288 | tf_op jit(solution)/shard_map/all_to_all | solution.py:11

commit v2 on v0

v2 whole, which is shorter than its diff:
```python
import functools

import jax
import jax.numpy as jnp
from jax import lax
from jax.experimental import pallas as pl
from jax.experimental.pallas import tpu as pltpu
from jax.sharding import Mesh, PartitionSpec as P

highest = lax.Precision.HIGHEST
ket_axes = ("zh", "zl", "y", "c")
swap_axes = ("c", "x", "zl", "y", "zh")
N, H, KB = 128, 64, 4
KL = H // KB
f32 = jnp.float32


def dot(a, b):
    return jnp.dot(a, b, precision=highest, preferred_element_type=f32)


def call(body, outs, *args, scratch=(), out_specs=None, name=None):
    vmem = pl.BlockSpec(memory_space=pltpu.VMEM)
    single = not isinstance(outs, list)
    outs_list = [outs] if single else list(outs)
    res = pl.pallas_call(
        body,
        out_shape=[jax.ShapeDtypeStruct(s, f32) for s in outs_list],
        in_specs=[vmem] * len(args),
        out_specs=[vmem] * len(outs_list),
        scratch_shapes=list(scratch),
        compiler_params=pltpu.CompilerParams(vmem_limit_bytes=40 * 2**20),
        name=name,
    )(*args)
    return res[0] if single else res


def prep_body(decay_ref, order_ref, turned_ref, nat_ref, til_ref, win_ref, rect_ref, shift_ref):
    decay = decay_ref[...]
    rows = lax.broadcasted_iota(jnp.int32, (N, N), 0)
    cols = lax.broadcasted_iota(jnp.int32, (N, N), 1)
    eye = (rows == cols).astype(f32)
    pick = (rows == order_ref[...]).astype(f32)
    pick_t = (rows == turned_ref[...]).astype(f32)
    nat = dot(pick.T, dot(decay, pick))
    til = dot(pick_t.T, dot(decay, pick_t))
    rect = dot(pick.T, dot(decay, pick_t))
    mean_full = jnp.sum(nat * eye) / N
    win = nat[:H, :H]
    mean_half = jnp.sum(win * eye[:H, :H]) / H
    nat_ref[...] = nat - mean_full * eye
    til_ref[...] = til - mean_full * eye
    win_ref[...] = win - mean_half * eye[:H, :H]
    rect_ref[...] = rect[:H, :]
    shift_ref[...] = jnp.full((1, N), 2.0 * (mean_full + mean_half), f32)


def send_body(x_ref, out_ref):
    for cb in range(8):
        out_ref[:, cb, :] = x_ref[cb * N : (cb + 1) * N, :].T


def middle_body(recv_ref, til_ref, win_ref, rect_ref, out_ref, flux_ref):
    parts = []
    for h in range(2):
        blocks = [
            recv_ref[:, kb, :, h, :].reshape(N, N).T.reshape(8, KL, N) for kb in range(KB)
        ]
        for j8 in range(8):
            parts.append(jnp.concatenate([b[j8] for b in blocks], axis=0))
    til, win = til_ref[...], win_ref[...]
    rect = rect_ref[...] * (1.0 / N)
    for c in range(16):
        flux_ref[c] = jnp.sum(parts[c] * rect, axis=0, keepdims=True)

    def outer(parts):
        tall = dot(jnp.concatenate(parts, axis=0), til)
        wide = dot(win, jnp.concatenate(parts, axis=1))
        return [
            tall[c * H : (c + 1) * H, :] + wide[:, c * N : (c + 1) * N] for c in range(16)
        ]

    for t in range(2):
        parts = outer(parts)
        for h in range(2):
            for kb in range(KB):
                block = jnp.concatenate(
                    [parts[h * 8 + j8][kb * KL : (kb + 1) * KL, :] for j8 in range(8)], axis=0
                )
                out_ref[:, kb, :, t * 2 + h, :] = block.T.reshape(2, 64, N)


def inner(src_ref, dst_ref, nat, win):
    wide = dot(win, jnp.concatenate([src_ref[pl.ds(k, H, stride=KL), :] for k in range(KL)], axis=1))
    for k in range(KL):
        dst_ref[pl.ds(k, H, stride=KL), :] = wide[:, k * N : (k + 1) * N]
    dst_ref[...] += dot(src_ref[...], nat)


def first_body(x_ref, nat_ref, win_ref, flux_ref, out_ref, pass_ref):
    pass_ref[...] = flux_ref[...]
    inner(x_ref, out_ref, nat_ref[...], win_ref[...])


def back_body(recv_ref, x_ref, rx_ref, nat_ref, win_ref, one_ref, two_ref, mom_ref, tmp_ref, res_ref):
    for cb in range(8):
        jg, h = divmod(cb, 2)
        rows = slice(cb * N, (cb + 1) * N)
        once = recv_ref[:, jg * 4 + h, :].T
        image = once + rx_ref[rows, :]
        one_ref[rows, :] = image
        tmp_ref[rows, :] = once + image
    inner(tmp_ref, res_ref, nat_ref[...], win_ref[...])
    sums = [jnp.zeros((8, N), f32) for _ in range(5)]
    for cb in range(8):
        jg, h = divmod(cb, 2)
        rows = slice(cb * N, (cb + 1) * N)
        two = recv_ref[:, jg * 4 + 2 + h, :].T + res_ref[rows, :]
        two_ref[rows, :] = two
        one, x = one_ref[rows, :], x_ref[rows, :]
        for q, (a, b) in enumerate([(x, x), (x, one), (one, one), (one, two), (two, two)]):
            sums[q] = sums[q] + jnp.sum((a * b).reshape(16, 8, N), axis=0)
    lane = lax.broadcasted_iota(jnp.int32, (1, N), 1)
    row = jnp.zeros((1, N), f32)
    for q in range(5):
        row = jnp.where(lane == q, jnp.sum(sums[q]), row)
    mom_ref[...] = jnp.broadcast_to(row[None], mom_ref.shape)


def relay_body(in_ref, out_ref):
    row = jnp.sum(in_ref[...], axis=0)
    out_ref[...] = jnp.broadcast_to(row[None], out_ref.shape)


def final_body(mom_ref, x_ref, one_ref, two_ref, shift_ref, out_ref, coef_ref, *, entries):
    row = jnp.sum(mom_ref[...], axis=0) / entries
    lane = lax.broadcasted_iota(jnp.int32, (1, N), 1)

    def mom(q):
        return jnp.broadcast_to(
            jnp.sum(jnp.where(lane == q, row, 0.0), axis=1, keepdims=True), (1, N)
        )

    m0, m1, m2, m3, m4 = [mom(q) for q in range(5)]
    shift = shift_ref[...]
    ratio = m1 / m0
    gap = m2 - ratio * m1
    theta = (m3 - 2.0 * ratio * m2 + ratio * ratio * m1) / gap
    slope = ratio + theta
    offset = theta * ratio - gap / m0
    size = jnp.sqrt(m4 - slope * m3 + offset * m2)
    b_one = 0.5 * jnp.sqrt(gap / m0)
    coefs = [
        -0.5 * (ratio + shift),
        b_one,
        b_one,
        -0.5 * (theta + shift),
        0.5 * size / jnp.sqrt(gap),
    ]
    line = jnp.zeros((1, N), f32)
    for q in range(5):
        line = jnp.where(lane == q, coefs[q], line)
    coef_ref[...] = line
    inv = 1.0 / size
    a, b = slope * inv, offset * inv
    out_ref[...] = two_ref[...] * inv - one_ref[...] * a + x_ref[...] * b


def swap(rows, axes=swap_axes):
    return lax.all_to_all(rows, axes, split_axis=0, concat_axis=0, tiled=True)


def shards(density, decay_matrix, atom_order):
    entries = float(N) * float(H) * float(H) * float(N)
    x = density.reshape(H * KL, N)
    turned_order = atom_order.reshape(4, 16, 2).transpose(2, 1, 0).reshape(1, N)
    nat, til, win, rect, shift = call(
        prep_body,
        [(N, N), (N, N), (H, H), (H, N), (1, N)],
        decay_matrix,
        atom_order.reshape(1, N),
        turned_order,
        name="prep",
    )
    sent = call(send_body, (N, 8, N), x, name="send")
    recv = swap(sent.reshape(512, 2, N)).reshape(2, KB, 64, 2, N)
    back, flux = call(
        middle_body, [(2, KB, 64, 4, N), (16, 1, N)], recv, til, win, rect, name="middle"
    )
    returned = swap(back.reshape(512, 4, N)).reshape(N, 16, N)
    rx, flux = call(first_body, [(H * KL, N), (16, 1, N)], x, nat, win, flux, name="first")
    flux = swap(flux, ("zl", "y"))
    returned, rx, flux = lax.optimization_barrier((returned, rx, flux))
    one, two, mom = call(
        back_body,
        [(H * KL, N), (H * KL, N), (32, 1, N)],
        returned,
        x,
        rx,
        nat,
        win,
        scratch=[pltpu.VMEM((H * KL, N), f32), pltpu.VMEM((H * KL, N), f32)],
        name="back",
    )
    mom = swap(mom, ("zh", "zl", "x"))
    mom = call(relay_body, (16, 1, N), mom, name="relay")
    mom = swap(mom, ("y", "c"))
    out, coef = call(
        functools.partial(final_body, entries=entries),
        [(H * KL, N), (1, N)],
        mom,
        x,
        one,
        two,
        shift,
        name="final",
    )
    return (out.reshape(density.shape), coef[0, :5], jnp.sum(flux, axis=(1, 2)))


def solution(mesh):
    fine = Mesh(mesh.devices.reshape(4, 2, 8, 2, 4), ket_axes + ("x",))
    return jax.shard_map(
        shards,
        mesh=fine,
        in_specs=(P(ket_axes, "x", None), P(), P()),
        out_specs=(P(ket_axes, "x", None), P(), P(ket_axes + ("x",))),
        check_vma=False,
    )
```

time: 693 us -> 135 us (0.19); the launches traced: 684 us -> 135 us
  blocking collectives: 484 us -> 68 us
  waiting for transfers between devices: 68.6 us -> 27.5 us
  local copies, waits for them, and re-layouts: 33.8 us -> 2 us
  other arithmetic: 31.4 us -> 0.71 us
  starting transfers between devices: 49.5 us -> 26.6 us
  matrix products: 12.3 us -> 0 us
  Pallas kernels: 0 us -> 8.99 us
    psum x5 -> x0, blocking collectives: 484 us -> none  [the longest x2 191 us: krylov_step(): lax.psum(jnp.sum(residual * residual), ('ket', 'blk')) / entries]
    all_to_all x0 -> x3, blocking collectives: none -> 68 us  [swap(): return lax.all_to_all(rows, axes, split_axis=0, concat_axis=0, tiled=True)]
    all_to_all x8 -> x2, waiting for transfers between devices: 68.6 us -> 27.5 us  [swap(): return lax.all_to_all(rows, axes, split_axis=0, concat_axis=0, tiled=True)]
    all_to_all x8 -> x0, other arithmetic: 23.8 us -> none  [the longest x2 6.65 us: liouvillian(): lax.all_to_all(ket_part(turned), 'ket', split_axis=0, concat_axis=1, tile...]
    all_to_all x8 -> x2, starting transfers between devices: 49.5 us -> 26.6 us  [swap(): return lax.all_to_all(rows, axes, split_axis=0, concat_axis=0, tiled=True)]
    unnamed x27 -> x8, local copies, waits for them, and re-layouts: 19.1 us -> 1.05 us
    dot_general x12 -> x0, matrix products: 12.3 us -> none  [the longest x2 4.4 us: bra_part(): mixed_rows = jnp.einsum('kb,pbc->pkc', window, turned, precision=highest)]
    pallas_call x0 -> x7, Pallas kernels: none -> 8.99 us  [call(): pl.pallas_call(body, out_shape=[jax.ShapeDtypeStruct(s, f32) for s in out...]
  transfers between devices with their start and end apart: 8 -> 2, of which waited for: 8 -> 2; matrix products, arithmetic and copies ran while one was open for 7% -> 1% of each run, Pallas kernels for 0% -> 0%
where the time goes in v2:
time: 135 us
  blocking collectives  68 us (50%)
  waiting for transfers between devices  27.5 us (20%)
  starting transfers between devices  26.6 us (20%)
  Pallas kernels  8.99 us (7%)
  local copies, waits for them, and re-layouts  2 us (1%)
    all_to_all x3, blocking collectives, swap(): return lax.all_to_all(rows, axes, split_axis=0, concat_axis=0, tiled=True)  68 us
    all_to_all x2, waiting for transfers between devices, swap(): return lax.all_to_all(rows, axes, split_axis=0, concat_axis=0, tiled=True)  27.5 us
    all_to_all x2, starting transfers between devices, swap(): return lax.all_to_all(rows, axes, split_axis=0, concat_axis=0, tiled=True)  26.6 us
    pallas_call x7, Pallas kernels, call(): pl.pallas_call(body, out_shape=[jax.ShapeDtypeStruct(s, f32) for s in out...  8.99 us
  transfers between devices with their start and end apart: 2, of which 2 were waited for; matrix products, arithmetic and copies ran while one was open for 1% of the time, Pallas kernels for 0%

profile of v2, /device:TPU:1, one launch (start us, length us, event | category | flops | bytes accessed | tf_op | source)
XLA Modules:
  0.0 134.5 jit_solution(9795961807083353138)
XLA Ops:
  0.6 0.0 copy-start
  0.6 1.0 copy-done
  1.7 1.1 send.1
  2.8 0.0 copy-start.3
  2.8 0.0 copy-start.2
  2.8 22.2 %all-to-all-start = ((f32[512,2,128]{2,1,0:T(2,128)}), f32[512,2,128]{2,1,0:T(2,128)S(1)}, u32[]{:S(2)}, u32[]{:S(2)}) async-start(f32[512,2,128]{2,1,0:T(2,128)} %bitcast.1), calls=%async_computation | async-start | bytes 1048576 | tf_op jit(solution)/shard_map/all_to_all | solution.py:170
  25.0 0.0 copy-done.3
  25.0 0.0 copy-start.1
  25.0 0.1 reshape.37
  25.2 0.2 copy.7
  25.4 0.1 reshape.38.turned_ref
  25.5 0.0 copy-done.2
  25.5 0.6 prep.1
  26.0 21.2 %all-to-all-done = f32[512,2,128]{2,1,0:T(2,128)S(1)} async-done(((f32[512,2,128]{2,1,0:T(2,128)}), f32[512,2,128]{2,1,0:T(2,128)S(1)}, u32[]{:S(2)}, u32[]{:S(2)}) %all-to-all-start) | async-done | bytes 524320 | tf_op jit(solution)/shard_map/all_to_all | solution.py:170
  47.2 2.4 %middle.1 = (f32[2,4,64,4,128]{4,3,2,1,0:T(4,128)S(1)}, f32[16,1,128]{2,1,0:T(1,128)S(1)}) custom-call(f32[2,4,64,2,128]{4,3,2,1,0:T(2,128)S(1)} %bitcast.15, f32[128,128]{1,0:T(8,128)S(1)} %get-tuple-element.20.til_ref, f32[64,64]{1,0:T(8,128)S(1)} %get-tuple-element.21.win_ref, f32[64,128]{1,0:T(8,128)S(1)} %get-tuple-element.22.rect_ref), custom_call_target="tpu_custom_call" | custom-call | tf_op jit(solution)/shard_map/middle/pallas_call | solution.py:26
  49.7 0.0 copy-done.1
  49.7 1.1 first.1
  50.8 10.4 %all_to_all.25 = f32[16,1,128]{2,1,0:T(1,128)S(1)} all-to-all(f32[16,1,128]{2,1,0:T(1,128)S(1)} %get-tuple-element.27), channel_id=1, replica_groups=mesh['zh'=4,'zl'=2,'y'=8,'c'=2,'x'=4] {'zl','y'}, dimensions={0} | all-to-all | bytes 16384 | tf_op jit(solution)/shard_map/all_to_all | solution.py:170
  61.3 43.4 %all_to_all.26 = f32[512,4,128]{2,1,0:T(4,128)S(1)} all-to-all(f32[512,4,128]{2,1,0:T(4,128)S(1)} %bitcast.16), channel_id=1, replica_groups=mesh['zh'=4,'zl'=2,'y'=8,'c'=2,'x'=4] {'c','x','zl','y','zh'}, dimensions={0} | all-to-all | bytes 2097152 | tf_op jit(solution)/shard_map/all_to_all | solution.py:170
  104.7 2.0 %back.1 = (f32[1024,128]{1,0:T(8,128)S(1)}, f32[1024,128]{1,0:T(8,128)S(1)}, f32[32,1,128]{2,1,0:T(1,128)S(1)}) custom-call(f32[128,16,128]{2,1,0:T(8,128)S(1)} %bitcast.14, f32[1024,128]{1,0:T(8,128)S(1)} %bitcast.12, f32[1024,128]{1,0:T(8,128)S(1)} %get-tuple-element.29.rx_ref, f32[128,128]{1,0:T(8,128)S(1)} %get-tuple-element.24.nat_ref, ...), custom_call_target="tpu_custom_call" | custom-call | tf_op jit(solution)/shard_map/back/pallas_call | solution.py:26
  106.7 14.1 %all_to_all.27.in_ref = f32[32,1,128]{2,1,0:T(1,128)S(1)} all-to-all(f32[32,1,128]{2,1,0:T(1,128)S(1)} %get-tuple-element.30), channel_id=1, replica_groups=mesh['zh'=4,'zl'=2,'y'=8,'c'=2,'x'=4] {'zh','zl','x'}, dimensions={0} | all-to-all | bytes 32768 | tf_op jit(solution)/shard_map/all_to_all | solution.py:170
  120.8 0.6 relay.1
  121.5 4.5 %all-to-all-start.4 = ((f32[16,1,128]{2,1,0:T(1,128)}), f32[16,1,128]{2,1,0:T(1,128)S(1)}, u32[]{:S(2)}, u32[]{:S(2)}) async-start(f32[16,1,128]{2,1,0:T(1,128)} %relay.1), calls=%async_computation.4 | async-start | bytes 16384 | tf_op jit(solution)/shard_map/all_to_all | solution.py:170
  125.9 0.7 reduce_sum.9
  126.6 6.3 %all-to-all-done.4.mom_ref = f32[16,1,128]{2,1,0:T(1,128)S(1)} async-done(((f32[16,1,128]{2,1,0:T(1,128)}), f32[16,1,128]{2,1,0:T(1,128)S(1)}, u32[]{:S(2)}, u32[]{:S(2)}) %all-to-all-start.4) | async-done | bytes 8224 | tf_op jit(solution)/shard_map/all_to_all | solution.py:170
  132.9 1.1 final.1
  134.0 0.5 slice_bitcast_fusion
Async XLA Ops:
  0.6 1.0 copy-start
  2.8 22.2 %copy-start.3 = (s32[128]{0:T(128)S(1)}, s32[128]{0:T(128)}, u32[]{:S(2)}) copy-start(s32[128]{0:T(128)} %param.5) | copy-start | bytes 1540
  2.8 22.6 %copy-start.2 = (f32[128,128]{1,0:T(8,128)S(1)}, f32[128,128]{1,0:T(8,128)}, u32[]{:S(2)}) copy-start(f32[128,128]{1,0:T(8,128)} %decay_ref.1) | copy-start | bytes 196612
  2.8 44.4 %all-to-all-start = ((f32[512,2,128]{2,1,0:T(2,128)}), f32[512,2,128]{2,1,0:T(2,128)S(1)}, u32[]{:S(2)}, u32[]{:S(2)}) async-start(f32[512,2,128]{2,1,0:T(2,128)} %bitcast.1), calls=%async_computation | async-start | bytes 1048576 | tf_op jit(solution)/shard_map/all_to_all | solution.py:170
  25.0 24.7 %copy-start.1 = (f32[64,16,128]{2,1,0:T(8,128)S(1)}, f32[64,16,128]{2,1,0:T(8,128)}, u32[]{:S(2)}) copy-start(f32[64,16,128]{2,1,0:T(8,128)} %param.3) | copy-start | bytes 1572868
  121.5 11.5 %all-to-all-start.4 = ((f32[16,1,128]{2,1,0:T(1,128)}), f32[16,1,128]{2,1,0:T(1,128)S(1)}, u32[]{:S(2)}, u32[]{:S(2)}) async-start(f32[16,1,128]{2,1,0:T(1,128)} %relay.1), calls=%async_computation.4 | async-start | bytes 16384 | tf_op jit(solution)/shard_map/all_to_all | solution.py:170

commit v3 on v2

--- a/solution.py
+++ b/solution.py
@@ -19,14 +19,18 @@
     return jnp.dot(a, b, precision=highest, preferred_element_type=f32)
 
 
-def call(body, outs, *args, scratch=(), out_specs=None, name=None):
+def call(body, outs, *args, scratch=(), scalar=None, name=None):
     vmem = pl.BlockSpec(memory_space=pltpu.VMEM)
+    in_specs = [vmem] * len(args)
+    if scalar is not None:
+        args = (scalar,) + args
+        in_specs = [pl.BlockSpec(memory_space=pltpu.SMEM)] + in_specs
     single = not isinstance(outs, list)
     outs_list = [outs] if single else list(outs)
     res = pl.pallas_call(
         body,
         out_shape=[jax.ShapeDtypeStruct(s, f32) for s in outs_list],
-        in_specs=[vmem] * len(args),
+        in_specs=in_specs,
         out_specs=[vmem] * len(outs_list),
         scratch_shapes=list(scratch),
         compiler_params=pltpu.CompilerParams(vmem_limit_bytes=40 * 2**20),
@@ -97,12 +101,17 @@
     dst_ref[...] += dot(src_ref[...], nat)
 
 
-def first_body(x_ref, nat_ref, win_ref, flux_ref, out_ref, pass_ref):
-    pass_ref[...] = flux_ref[...]
+def first_body(x_ref, nat_ref, win_ref, out_ref):
     inner(x_ref, out_ref, nat_ref[...], win_ref[...])
 
 
-def back_body(recv_ref, x_ref, rx_ref, nat_ref, win_ref, one_ref, two_ref, mom_ref, tmp_ref, res_ref):
+def place(where):
+    return where // 128, (where // 64) % 2, (where // 8) % 8, (where // 4) % 2, where % 4
+
+
+def back_body(
+    where_ref, recv_ref, x_ref, rx_ref, nat_ref, win_ref, flux_ref, one_ref, two_ref, mom_ref, tmp_ref, res_ref
+):
     for cb in range(8):
         jg, h = divmod(cb, 2)
         rows = slice(cb * N, (cb + 1) * N)
@@ -124,7 +133,19 @@
     row = jnp.zeros((1, N), f32)
     for q in range(5):
         row = jnp.where(lane == q, jnp.sum(sums[q]), row)
-    mom_ref[...] = jnp.broadcast_to(row[None], mom_ref.shape)
+    zh, zl, _, _, xi = place(where_ref[0])
+    flux = jnp.sum(flux_ref[...].reshape(16, N), axis=1, keepdims=True)
+    spot = lax.broadcasted_iota(jnp.int32, (8, N), 1) == (
+        lax.broadcasted_iota(jnp.int32, (8, N), 0) + 8 + 8 * zl
+    )
+    dest = lax.broadcasted_iota(jnp.int32, (4, 1, N), 0)
+    for group in range(2):
+        mine = jnp.sum(
+            jnp.where(spot, flux[8 * group : 8 * group + 8], 0.0), axis=0, keepdims=True
+        )
+        for q in range(4):
+            kept = jnp.where((dest == xi) & (zh == q), mine[None], 0.0)
+            mom_ref[pl.ds(q * 8 + group * 4, 4)] = row[None] + kept
 
 
 def relay_body(in_ref, out_ref):
@@ -132,8 +153,25 @@
     out_ref[...] = jnp.broadcast_to(row[None], out_ref.shape)
 
 
-def final_body(mom_ref, x_ref, one_ref, two_ref, shift_ref, out_ref, coef_ref, *, entries):
-    row = jnp.sum(mom_ref[...], axis=0) / entries
+def final_body(
+    where_ref, mom_ref, x_ref, one_ref, two_ref, shift_ref, out_ref, coef_ref, flux_ref, *, entries
+):
+    got = mom_ref[...].reshape(16, N)
+    _, _, y, c, _ = place(where_ref[0])
+    lanes = lax.broadcasted_iota(jnp.int32, (16, N), 1)
+    source = lax.broadcasted_iota(jnp.int32, (16, N), 0)
+    flux = jnp.zeros((1, N), f32)
+    for zl in range(2):
+        entry = jnp.sum(
+            jnp.where((lanes == 8 + 8 * zl + y) & (source % 2 == c), got, 0.0),
+            axis=1,
+            keepdims=True,
+        )
+        flux += jnp.sum(
+            jnp.where(lanes == 8 * zl + source // 2, entry, 0.0), axis=0, keepdims=True
+        )
+    flux_ref[...] = flux[:, :16]
+    row = jnp.sum(got, axis=0, keepdims=True) / entries
     lane = lax.broadcasted_iota(jnp.int32, (1, N), 1)
 
     def mom(q):
@@ -160,7 +198,7 @@
     line = jnp.zeros((1, N), f32)
     for q in range(5):
         line = jnp.where(lane == q, coefs[q], line)
-    coef_ref[...] = line
+    coef_ref[...] = line[:, :5]
     inv = 1.0 / size
     a, b = slope * inv, offset * inv
     out_ref[...] = two_ref[...] * inv - one_ref[...] * a + x_ref[...] * b
@@ -182,15 +220,15 @@
         turned_order,
         name="prep",
     )
+    where = lax.axis_index(ket_axes + ("x",)).astype(jnp.int32).reshape(1)
     sent = call(send_body, (N, 8, N), x, name="send")
     recv = swap(sent.reshape(512, 2, N)).reshape(2, KB, 64, 2, N)
+    rx = call(first_body, (H * KL, N), x, nat, win, name="first")
+    recv, rx, where = lax.optimization_barrier((recv, rx, where))
     back, flux = call(
         middle_body, [(2, KB, 64, 4, N), (16, 1, N)], recv, til, win, rect, name="middle"
     )
     returned = swap(back.reshape(512, 4, N)).reshape(N, 16, N)
-    rx, flux = call(first_body, [(H * KL, N), (16, 1, N)], x, nat, win, flux, name="first")
-    flux = swap(flux, ("zl", "y"))
-    returned, rx, flux = lax.optimization_barrier((returned, rx, flux))
     one, two, mom = call(
         back_body,
         [(H * KL, N), (H * KL, N), (32, 1, N)],
@@ -199,23 +237,26 @@
         rx,
         nat,
         win,
+        flux,
         scratch=[pltpu.VMEM((H * KL, N), f32), pltpu.VMEM((H * KL, N), f32)],
+        scalar=where,
         name="back",
     )
     mom = swap(mom, ("zh", "zl", "x"))
     mom = call(relay_body, (16, 1, N), mom, name="relay")
     mom = swap(mom, ("y", "c"))
-    out, coef = call(
+    out, coef, flux = call(
         functools.partial(final_body, entries=entries),
-        [(H * KL, N), (1, N)],
+        [(H * KL, N), (1, 5), (1, 16)],
         mom,
         x,
         one,
         two,
         shift,
+        scalar=where,
         name="final",
     )
-    return (out.reshape(density.shape), coef[0, :5], jnp.sum(flux, axis=(1, 2)))
+    return out.reshape(density.shape), coef.reshape(5), flux.reshape(16)
 
 
 def solution(mesh):

time: 135 us -> 120 us (0.89)
  waiting for transfers between devices: 27.5 us -> 19.4 us
  starting transfers between devices: 26.6 us -> 22.2 us
  blocking collectives: 68 us -> 66.4 us
    all_to_all x2 -> x1, waiting for transfers between devices: 27.5 us -> 19.4 us  [swap(): return lax.all_to_all(rows, axes, split_axis=0, concat_axis=0, tiled=True)]
    all_to_all x2 -> x1, starting transfers between devices: 26.6 us -> 22.2 us  [swap(): return lax.all_to_all(rows, axes, split_axis=0, concat_axis=0, tiled=True)]
    all_to_all x3, blocking collectives: 68 us -> 66.4 us  [swap(): return lax.all_to_all(rows, axes, split_axis=0, concat_axis=0, tiled=True)]
  transfers between devices with their start and end apart: 2 -> 1, of which waited for: 2 -> 1; matrix products, arithmetic and copies ran while one was open for 1% -> 0% of each run, Pallas kernels for 0% -> 1%
where the time goes in v3:
time: 120 us; the launch traced here: 119 us
  blocking collectives  66.4 us (55%)
  starting transfers between devices  22.2 us (18%)
  waiting for transfers between devices  19.4 us (16%)
  Pallas kernels  8.52 us (7%)
  local copies, waits for them, and re-layouts  2.12 us (2%)
    all_to_all x3, blocking collectives, swap(): return lax.all_to_all(rows, axes, split_axis=0, concat_axis=0, tiled=True)  66.4 us
    all_to_all x1, starting transfers between devices, swap(): return lax.all_to_all(rows, axes, split_axis=0, concat_axis=0, tiled=True)  22.2 us
    all_to_all x1, waiting for transfers between devices, swap(): return lax.all_to_all(rows, axes, split_axis=0, concat_axis=0, tiled=True)  19.4 us
    pallas_call x7, Pallas kernels, call(): pl.pallas_call(body, out_shape=[jax.ShapeDtypeStruct(s, f32) for s in out...  8.52 us
  transfers between devices with their start and end apart: 1, of which 1 were waited for; matrix products, arithmetic and copies ran while one was open for 0% of the time, Pallas kernels for 1%

profile of v3, /device:TPU:1, one launch (start us, length us, event | category | flops | bytes accessed | tf_op | source)
XLA Modules:
  0.0 119.3 jit_solution(9085383941463511332)
XLA Ops:
  0.6 0.0 copy-start
  0.6 1.0 copy-done
  1.7 1.1 send.1
  2.8 0.0 copy-start.1
  2.8 22.2 %all-to-all-start = ((f32[512,2,128]{2,1,0:T(2,128)}), f32[512,2,128]{2,1,0:T(2,128)S(1)}, u32[]{:S(2)}, u32[]{:S(2)}) async-start(f32[512,2,128]{2,1,0:T(2,128)} %bitcast.1), calls=%async_computation | async-start | bytes 1048576 | tf_op jit(solution)/shard_map/all_to_all | solution.py:208
  25.0 0.0 copy-start.3
  25.0 0.0 copy-start.2
  25.0 0.6 copy-done.3
  25.7 0.1 reshape.46
  25.8 0.2 copy.7
  26.0 0.1 reshape.47.turned_ref
  26.1 0.0 copy-done.2
  26.1 0.6 prep.1
  26.7 0.0 copy-done.1
  26.7 1.1 first.1.rx_ref
  27.9 19.4 %all-to-all-done = f32[512,2,128]{2,1,0:T(2,128)S(1)} async-done(((f32[512,2,128]{2,1,0:T(2,128)}), f32[512,2,128]{2,1,0:T(2,128)S(1)}, u32[]{:S(2)}, u32[]{:S(2)}) %all-to-all-start) | async-done | bytes 524320 | tf_op jit(solution)/shard_map/all_to_all | solution.py:208
  47.2 2.4 %middle.1 = (f32[2,4,64,4,128]{4,3,2,1,0:T(4,128)S(1)}, f32[16,1,128]{2,1,0:T(1,128)S(1)}) custom-call(f32[2,4,64,2,128]{4,3,2,1,0:T(2,128)S(1)} %bitcast.16, f32[128,128]{1,0:T(8,128)S(1)} %get-tuple-element.23.til_ref, f32[64,64]{1,0:T(8,128)S(1)} %get-tuple-element.20.win_ref, f32[64,128]{1,0:T(8,128)S(1)} %get-tuple-element.24.rect_ref), custom_call_target="tpu_custom_call" | custom-call | tf_op jit(solution)/shard_map/middle/pallas_call | solution.py:30
  49.7 41.6 %all_to_all.20 = f32[512,4,128]{2,1,0:T(4,128)S(1)} all-to-all(f32[512,4,128]{2,1,0:T(4,128)S(1)} %bitcast.17), channel_id=1, replica_groups=mesh['zh'=4,'zl'=2,'y'=8,'c'=2,'x'=4] {'c','x','zl','y','zh'}, dimensions={0} | all-to-all | bytes 2097152 | tf_op jit(solution)/shard_map/all_to_all | solution.py:208
  91.3 2.1 %back.1 = (f32[1024,128]{1,0:T(8,128)S(1)}, f32[1024,128]{1,0:T(8,128)S(1)}, f32[32,1,128]{2,1,0:T(1,128)S(1)}) custom-call(s32[1]{0:T(128)} %bitcast.5.where_ref, f32[128,16,128]{2,1,0:T(8,128)S(1)} %bitcast.15, f32[1024,128]{1,0:T(8,128)S(1)} %bitcast.13, f32[1024,128]{1,0:T(8,128)S(1)} %first.1.rx_ref, f32[128,128]{1,0:T(8,128)S(1)} %get-tuple-element.19.nat_ref, ...), custom_call_target="tpu_custom_call" | custom-call | tf_op jit(solution)/shard_map/back/pallas_call | solution.py:30
  93.4 14.1 %all_to_all.21.in_ref = f32[32,1,128]{2,1,0:T(1,128)S(1)} all-to-all(f32[32,1,128]{2,1,0:T(1,128)S(1)} %get-tuple-element.28), channel_id=1, replica_groups=mesh['zh'=4,'zl'=2,'y'=8,'c'=2,'x'=4] {'zh','zl','x'}, dimensions={0} | all-to-all | bytes 32768 | tf_op jit(solution)/shard_map/all_to_all | solution.py:208
  107.5 10.7 %all_to_all.22.mom_ref = f32[16,1,128]{2,1,0:T(1,128)S(1)} all-to-all(f32[16,1,128]{2,1,0:T(1,128)S(1)} %relay.1), channel_id=1, replica_groups=mesh['zh'=4,'zl'=2,'y'=8,'c'=2,'x'=4] {'y','c'}, dimensions={0} | all-to-all | bytes 16384 | tf_op jit(solution)/shard_map/all_to_all | solution.py:208
  118.2 1.1 final.1
  (1 shorter events, 0.0 us)
Async XLA Ops:
  0.6 1.0 copy-start
  2.8 23.9 %copy-start.1 = (f32[64,16,128]{2,1,0:T(8,128)S(1)}, f32[64,16,128]{2,1,0:T(8,128)}, u32[]{:S(2)}) copy-start(f32[64,16,128]{2,1,0:T(8,128)} %param.3) | copy-start | bytes 1572868
  2.8 44.4 %all-to-all-start = ((f32[512,2,128]{2,1,0:T(2,128)}), f32[512,2,128]{2,1,0:T(2,128)S(1)}, u32[]{:S(2)}, u32[]{:S(2)}) async-start(f32[512,2,128]{2,1,0:T(2,128)} %bitcast.1), calls=%async_computation | async-start | bytes 1048576 | tf_op jit(solution)/shard_map/all_to_all | solution.py:208
  25.0 0.7 copy-start.3
  25.0 1.1 copy-start.2

commit v4 on v3

--- a/solution.py
+++ b/solution.py
@@ -19,9 +19,10 @@
     return jnp.dot(a, b, precision=highest, preferred_element_type=f32)
 
 
-def call(body, outs, *args, scratch=(), scalar=None, name=None):
+def call(body, outs, *args, scratch=(), scalar=None, name=None, raw_in=False, raw_out=False):
     vmem = pl.BlockSpec(memory_space=pltpu.VMEM)
-    in_specs = [vmem] * len(args)
+    raw = pl.BlockSpec(memory_space=pltpu.HBM)
+    in_specs = [raw if raw_in else vmem] * len(args)
     if scalar is not None:
         args = (scalar,) + args
         in_specs = [pl.BlockSpec(memory_space=pltpu.SMEM)] + in_specs
@@ -31,7 +32,7 @@
         body,
         out_shape=[jax.ShapeDtypeStruct(s, f32) for s in outs_list],
         in_specs=in_specs,
-        out_specs=[vmem] * len(outs_list),
+        out_specs=[raw if raw_out else vmem] + [vmem] * (len(outs_list) - 1),
         scratch_shapes=list(scratch),
         compiler_params=pltpu.CompilerParams(vmem_limit_bytes=40 * 2**20),
         name=name,
@@ -59,9 +60,15 @@
     shift_ref[...] = jnp.full((1, N), 2.0 * (mean_full + mean_half), f32)
 
 
-def send_body(x_ref, out_ref):
+def send_body(x_ref, out_ref, buf_ref, sem):
+    copies = []
     for cb in range(8):
-        out_ref[:, cb, :] = x_ref[cb * N : (cb + 1) * N, :].T
+        rows = pl.ds(cb * N, N)
+        copies.append(pltpu.make_async_copy(x_ref.at[rows], buf_ref.at[rows], sem.at[cb]))
+        copies[-1].start()
+    for cb in range(8):
+        copies[cb].wait()
+        out_ref[:, cb, :] = buf_ref[cb * N : (cb + 1) * N, :].T
 
 
 def middle_body(recv_ref, til_ref, win_ref, rect_ref, out_ref, flux_ref):
@@ -154,23 +161,21 @@
 
 
 def final_body(
-    where_ref, mom_ref, x_ref, one_ref, two_ref, shift_ref, out_ref, coef_ref, flux_ref, *, entries
+    where_ref,
+    mom_ref,
+    x_ref,
+    one_ref,
+    two_ref,
+    shift_ref,
+    out_ref,
+    coef_ref,
+    flux_ref,
+    buf_ref,
+    sem,
+    *,
+    entries,
 ):
     got = mom_ref[...].reshape(16, N)
-    _, _, y, c, _ = place(where_ref[0])
-    lanes = lax.broadcasted_iota(jnp.int32, (16, N), 1)
-    source = lax.broadcasted_iota(jnp.int32, (16, N), 0)
-    flux = jnp.zeros((1, N), f32)
-    for zl in range(2):
-        entry = jnp.sum(
-            jnp.where((lanes == 8 + 8 * zl + y) & (source % 2 == c), got, 0.0),
-            axis=1,
-            keepdims=True,
-        )
-        flux += jnp.sum(
-            jnp.where(lanes == 8 * zl + source // 2, entry, 0.0), axis=0, keepdims=True
-        )
-    flux_ref[...] = flux[:, :16]
     row = jnp.sum(got, axis=0, keepdims=True) / entries
     lane = lax.broadcasted_iota(jnp.int32, (1, N), 1)
 
@@ -195,13 +200,34 @@
         -0.5 * (theta + shift),
         0.5 * size / jnp.sqrt(gap),
     ]
+    inv = 1.0 / size
+    a, b = slope * inv, offset * inv
+    copies = []
+    for cb in range(4):
+        rows = pl.ds(cb * 2 * N, 2 * N)
+        buf_ref[rows, :] = two_ref[rows, :] * inv - one_ref[rows, :] * a + x_ref[rows, :] * b
+        copies.append(pltpu.make_async_copy(buf_ref.at[rows], out_ref.at[rows], sem.at[cb]))
+        copies[-1].start()
     line = jnp.zeros((1, N), f32)
     for q in range(5):
         line = jnp.where(lane == q, coefs[q], line)
     coef_ref[...] = line[:, :5]
-    inv = 1.0 / size
-    a, b = slope * inv, offset * inv
-    out_ref[...] = two_ref[...] * inv - one_ref[...] * a + x_ref[...] * b
+    _, _, y, c, _ = place(where_ref[0])
+    lanes = lax.broadcasted_iota(jnp.int32, (16, N), 1)
+    source = lax.broadcasted_iota(jnp.int32, (16, N), 0)
+    flux = jnp.zeros((1, N), f32)
+    for zl in range(2):
+        entry = jnp.sum(
+            jnp.where((lanes == 8 + 8 * zl + y) & (source % 2 == c), got, 0.0),
+            axis=1,
+            keepdims=True,
+        )
+        flux += jnp.sum(
+            jnp.where(lanes == 8 * zl + source // 2, entry, 0.0), axis=0, keepdims=True
+        )
+    flux_ref[...] = flux[:, :16]
+    for copy in copies:
+        copy.wait()
 
 
 def swap(rows, axes=swap_axes):
@@ -221,7 +247,14 @@
         name="prep",
     )
     where = lax.axis_index(ket_axes + ("x",)).astype(jnp.int32).reshape(1)
-    sent = call(send_body, (N, 8, N), x, name="send")
+    sent = call(
+        send_body,
+        (N, 8, N),
+        x,
+        scratch=[pltpu.VMEM((H * KL, N), f32), pltpu.SemaphoreType.DMA((8,))],
+        raw_in=True,
+        name="send",
+    )
     recv = swap(sent.reshape(512, 2, N)).reshape(2, KB, 64, 2, N)
     rx = call(first_body, (H * KL, N), x, nat, win, name="first")
     recv, rx, where = lax.optimization_barrier((recv, rx, where))
@@ -253,7 +286,9 @@
         one,
         two,
         shift,
+        scratch=[pltpu.VMEM((H * KL, N), f32), pltpu.SemaphoreType.DMA((4,))],
         scalar=where,
+        raw_out=True,
         name="final",
     )
     return out.reshape(density.shape), coef.reshape(5), flux.reshape(16)

time: 120 us -> 121 us (level)
  Pallas kernels: 8.52 us -> 10.2 us
    pallas_call x7, Pallas kernels: 8.52 us -> 10.2 us  [call(): pl.pallas_call(body, out_shape=[jax.ShapeDtypeStruct(s, f32) for s in out...]
where the time goes in v4:
time: 121 us
  blocking collectives  66.4 us (55%)
  starting transfers between devices  22.2 us (18%)
  waiting for transfers between devices  19.4 us (16%)
  Pallas kernels  10.2 us (8%)
  local copies, waits for them, and re-layouts  2.12 us (2%)
    all_to_all x3, blocking collectives, swap(): return lax.all_to_all(rows, axes, split_axis=0, concat_axis=0, tiled=True)  66.4 us
    all_to_all x1, starting transfers between devices, swap(): return lax.all_to_all(rows, axes, split_axis=0, concat_axis=0, tiled=True)  22.2 us
    all_to_all x1, waiting for transfers between devices, swap(): return lax.all_to_all(rows, axes, split_axis=0, concat_axis=0, tiled=True)  19.4 us
    pallas_call x7, Pallas kernels, call(): pl.pallas_call(body, out_shape=[jax.ShapeDtypeStruct(s, f32) for s in out...  10.2 us
  transfers between devices with their start and end apart: 1, of which 1 were waited for; matrix products, arithmetic and copies ran while one was open for 0% of the time, Pallas kernels for 1%

profile of v4, /device:TPU:1, one launch (start us, length us, event | category | flops | bytes accessed | tf_op | source)
XLA Modules:
  0.0 121.1 jit_solution(10044588790141282499)
XLA Ops:
  0.6 0.0 copy-start
  0.6 1.0 copy-done
  1.7 2.4 %send.1 = f32[128,8,128]{2,1,0:T(8,128)} custom-call(f32[1024,128]{1,0:T(8,128)S(1)} %bitcast.11), custom_call_target="tpu_custom_call" | custom-call | tf_op jit(solution)/shard_map/send/pallas_call | solution.py:31
  4.1 0.0 copy-start.1
  4.1 22.2 %all-to-all-start = ((f32[512,2,128]{2,1,0:T(2,128)}), f32[512,2,128]{2,1,0:T(2,128)S(1)}, u32[]{:S(2)}, u32[]{:S(2)}) async-start(f32[512,2,128]{2,1,0:T(2,128)} %bitcast.1), calls=%async_computation | async-start | bytes 1048576 | tf_op jit(solution)/shard_map/all_to_all | solution.py:234
  26.3 0.0 copy-start.3
  26.3 0.0 copy-start.2
  26.3 0.6 copy-done.3
  26.9 0.1 reshape.46
  27.0 0.2 copy.7
  27.2 0.1 reshape.47.turned_ref
  27.4 0.0 copy-done.2
  27.4 0.6 prep.1
  28.0 0.0 copy-done.1
  28.0 1.1 first.1.rx_ref
  29.1 19.4 %all-to-all-done = f32[512,2,128]{2,1,0:T(2,128)S(1)} async-done(((f32[512,2,128]{2,1,0:T(2,128)}), f32[512,2,128]{2,1,0:T(2,128)S(1)}, u32[]{:S(2)}, u32[]{:S(2)}) %all-to-all-start) | async-done | bytes 524320 | tf_op jit(solution)/shard_map/all_to_all | solution.py:234
  48.5 2.4 %middle.1 = (f32[2,4,64,4,128]{4,3,2,1,0:T(4,128)S(1)}, f32[16,1,128]{2,1,0:T(1,128)S(1)}) custom-call(f32[2,4,64,2,128]{4,3,2,1,0:T(2,128)S(1)} %bitcast.16, f32[128,128]{1,0:T(8,128)S(1)} %get-tuple-element.23.til_ref, f32[64,64]{1,0:T(8,128)S(1)} %get-tuple-element.20.win_ref, f32[64,128]{1,0:T(8,128)S(1)} %get-tuple-element.24.rect_ref), custom_call_target="tpu_custom_call" | custom-call | tf_op jit(solution)/shard_map/middle/pallas_call | solution.py:31
  50.9 41.6 %all_to_all.20 = f32[512,4,128]{2,1,0:T(4,128)S(1)} all-to-all(f32[512,4,128]{2,1,0:T(4,128)S(1)} %bitcast.17), channel_id=1, replica_groups=mesh['zh'=4,'zl'=2,'y'=8,'c'=2,'x'=4] {'c','x','zl','y','zh'}, dimensions={0} | all-to-all | bytes 2097152 | tf_op jit(solution)/shard_map/all_to_all | solution.py:234
  92.5 2.1 %back.1 = (f32[1024,128]{1,0:T(8,128)S(1)}, f32[1024,128]{1,0:T(8,128)S(1)}, f32[32,1,128]{2,1,0:T(1,128)S(1)}) custom-call(s32[1]{0:T(128)} %bitcast.5.where_ref, f32[128,16,128]{2,1,0:T(8,128)S(1)} %bitcast.15, f32[1024,128]{1,0:T(8,128)S(1)} %bitcast.13, f32[1024,128]{1,0:T(8,128)S(1)} %first.1.rx_ref, f32[128,128]{1,0:T(8,128)S(1)} %get-tuple-element.19.nat_ref, ...), custom_call_target="tpu_custom_call" | custom-call | tf_op jit(solution)/shard_map/back/pallas_call | solution.py:31
  94.6 14.1 %all_to_all.21.in_ref = f32[32,1,128]{2,1,0:T(1,128)S(1)} all-to-all(f32[32,1,128]{2,1,0:T(1,128)S(1)} %get-tuple-element.28), channel_id=1, replica_groups=mesh['zh'=4,'zl'=2,'y'=8,'c'=2,'x'=4] {'zh','zl','x'}, dimensions={0} | all-to-all | bytes 32768 | tf_op jit(solution)/shard_map/all_to_all | solution.py:234
  108.8 10.7 %all_to_all.22.mom_ref = f32[16,1,128]{2,1,0:T(1,128)S(1)} all-to-all(f32[16,1,128]{2,1,0:T(1,128)S(1)} %relay.1), channel_id=1, replica_groups=mesh['zh'=4,'zl'=2,'y'=8,'c'=2,'x'=4] {'y','c'}, dimensions={0} | all-to-all | bytes 16384 | tf_op jit(solution)/shard_map/all_to_all | solution.py:234
  119.5 1.5 %final.1 = (f32[1024,128]{1,0:T(8,128)}, f32[1,5]{1,0:T(1,128)}, f32[1,16]{1,0:T(1,128)}) custom-call(s32[1]{0:T(128)} %bitcast.5.where_ref, f32[16,1,128]{2,1,0:T(1,128)S(1)} %all_to_all.22.mom_ref, f32[1024,128]{1,0:T(8,128)S(1)} %bitcast.14, f32[1024,128]{1,0:T(8,128)S(1)} %get-tuple-element.29.one_ref, f32[1024,128]{1,0:T(8,128)S(1)} %get-tuple-element.30.two_ref, ...), custom_call_target="tpu_custom_call" | custom-call | tf_op jit(solution)/shard_map/final/pallas_call | solution.py:31
  (1 shorter events, 0.0 us)
Async XLA Ops:
  0.6 1.0 copy-start
  4.1 23.9 %copy-start.1 = (f32[64,16,128]{2,1,0:T(8,128)S(1)}, f32[64,16,128]{2,1,0:T(8,128)}, u32[]{:S(2)}) copy-start(f32[64,16,128]{2,1,0:T(8,128)} %param.3) | copy-start | bytes 1572868
  4.1 44.4 %all-to-all-start = ((f32[512,2,128]{2,1,0:T(2,128)}), f32[512,2,128]{2,1,0:T(2,128)S(1)}, u32[]{:S(2)}, u32[]{:S(2)}) async-start(f32[512,2,128]{2,1,0:T(2,128)} %bitcast.1), calls=%async_computation | async-start | bytes 1048576 | tf_op jit(solution)/shard_map/all_to_all | solution.py:234
  26.3 0.7 copy-start.3
  26.3 1.1 copy-start.2
